TPU v7x, 32 devices: a whole 2x2x4 slice. The times are simulated.
32 devices in a mesh: node: 4 (over z), grp: 2 (over y), rep: 4 (over x, core).
Axes of the slice: x: 2, y: 2, z: 4, core: 2. Of those that a mesh axis runs over, the one named last changes fastest.
Arguments:
- tokens: bfloat16 [1024, 768], P(('node', 'grp'), 'rep'), may hold values from -6 to 6
- gates: float32 [1024, 2], P(('node', 'grp')), may hold values from 0.05 to 1
- expert_ids: int32 [1024, 2], P(('node', 'grp')), may hold values from 0 to 7, all different within a row; in each aligned block of 128 rows (0 to 127, 128 to 255, ...) at most 64 rows name the same one
- w_in: bfloat16 [8, 768, 1536], P(('node', 'grp'), None, 'rep'), may hold values from -0.21875 to 0.21875
- b_in: float32 [8, 1536], P(('node', 'grp'), 'rep'), may hold values from -3 to 3
- w_out: bfloat16 [8, 1536, 768], P(('node', 'grp'), 'rep'), may hold values from -0.15625 to 0.15625
- b_out: float32 [8, 768], P(('node', 'grp'), 'rep'), may hold values from -3 to 3
- cotangent: bfloat16 [1024, 768], P(('node', 'grp'), 'rep'), may hold values from -6 to 6
Outputs:
- mixed: bfloat16 [1024, 768], P(('node', 'grp'), 'rep')
- d_tokens: bfloat16 [1024, 768], P(('node', 'grp'), 'rep')
- d_gates: float32 [1024, 2], P(('node', 'grp'))
- d_w_in: float32 [8, 768, 1536], P(('node', 'grp'), None, 'rep')
- d_b_in: float32 [8, 1536], P(('node', 'grp'), 'rep')
- d_w_out: float32 [8, 1536, 768], P(('node', 'grp'), 'rep')
- d_b_out: float32 [8, 768], P(('node', 'grp'), 'rep')
Inputs may be any that keep to these rules, and one draw needn't show every extreme that they name: `expert_ids`: each row names 2 different experts. Among the 128 rows of one device's aligned block no expert is named more than 64 times, and in some blocks one expert is named exactly 64 times.
All inputs are finite; a program needn't handle non-finite values.
Results may differ from a plain program's by a relative error of at most 0.0064.
Values may be sent and summed in bfloat16 or wider, within the bound.
No kernel may reach another device: no remote copies, remote signals or barrier semaphores. Data moves between devices by JAX's collectives and lax.ppermute only.
A program may use at most 64 MiB of HBM per device.

v0:
```python
import jax
import jax.numpy as jnp
from jax import lax
from jax.sharding import PartitionSpec as P


def contract_first(left, right):
    return lax.dot_general(
        left, right, (((0,), (0,)), ((), ())), preferred_element_type=jnp.float32
    )


def contract_last(left, right):
    return lax.dot_general(
        left, right, (((1,), (1,)), ((), ())), preferred_element_type=jnp.float32
    )


def relocate(buffer):
    return lax.all_to_all(buffer, ("node", "grp"), split_axis=0, concat_axis=0, tiled=True)


def per_device(tokens, gates, expert_ids, w_in, b_in, w_out, b_out, cotangent):
    n_experts = lax.axis_size(("node", "grp"))
    tok_rows, feat_width = tokens.shape
    top_k = expert_ids.shape[1]
    assigned = tok_rows * top_k
    capacity = max(2, 2 * assigned // n_experts)
    rows_total = n_experts * capacity
    flat_ids = expert_ids.reshape(assigned)
    position = jnp.arange(assigned, dtype=jnp.int32)
    matches = (flat_ids[:, None] == flat_ids[None, :]) & (position[None, :] < position[:, None])
    slot_rank = jnp.sum(matches.astype(jnp.int32), axis=1)
    target = flat_ids * capacity + slot_rank
    placing = (jnp.arange(rows_total, dtype=jnp.int32)[:, None] == target[None, :]).astype(
        jnp.bfloat16
    )
    token_copies = jnp.repeat(tokens, top_k, axis=0)
    outbound = jnp.dot(placing, token_copies, preferred_element_type=jnp.float32).astype(
        jnp.bfloat16
    )
    inbound = relocate(outbound.reshape(n_experts, capacity, feat_width))
    expert_x = inbound.reshape(rows_total, feat_width)
    w_first = w_in[0]
    bias_first = b_in[0]
    w_second = w_out[0]
    bias_second = b_out[0]
    feat_local = w_second.shape[1] // lax.axis_size("rep")
    full_x = lax.all_gather(expert_x, "rep", axis=1, tiled=True)
    pre_act = jnp.dot(full_x, w_first, preferred_element_type=jnp.float32)
    pre_act = pre_act + bias_first
    hidden = jax.nn.gelu(pre_act).astype(jnp.bfloat16)
    second_block = lax.all_to_all(w_second, "rep", split_axis=1, concat_axis=0, tiled=True)
    weights = second_block
    summed = jnp.dot(
        lax.all_gather(hidden, "rep", axis=1, tiled=True),
        weights,
        preferred_element_type=jnp.float32,
    )
    expert_out = (summed + bias_second).astype(jnp.bfloat16)
    returned = relocate(expert_out.reshape(n_experts, capacity, feat_local)).reshape(
        rows_total, feat_local
    )
    per_assign = contract_first(placing, returned).reshape(tok_rows, top_k, feat_local)
    mixed = jnp.sum(gates[:, :, None] * per_assign, axis=1).astype(jnp.bfloat16)
    cot_wide = cotangent.astype(jnp.float32)
    gate_terms = jnp.sum(cot_wide[:, None, :] * per_assign, axis=2)
    d_gates = lax.psum(gate_terms, "rep")
    d_out = (
        (gates[:, :, None] * cot_wide[:, None, :])
        .astype(jnp.bfloat16)
        .reshape(assigned, feat_width)
    )
    grad_outbound = jnp.dot(placing, d_out, preferred_element_type=jnp.float32).astype(jnp.bfloat16)
    expert_grad = relocate(grad_outbound.reshape(n_experts, capacity, feat_width)).reshape(
        rows_total, feat_width
    )
    grad_bias_out = jnp.sum(expert_grad.astype(jnp.float32), axis=0)
    full_grad = lax.all_gather(expert_grad, "rep", axis=1, tiled=True)
    grad_w_out = contract_first(hidden, full_grad)
    d_hidden = contract_last(full_grad, w_second)
    _, pull_back = jax.vjp(jax.nn.gelu, pre_act)
    d_pre = pull_back(d_hidden)[0].astype(jnp.bfloat16)
    grad_bias_in = jnp.sum(d_pre.astype(jnp.float32), axis=0)
    grad_w_in = contract_first(full_x, d_pre)
    first_block = lax.all_to_all(w_first, "rep", split_axis=0, concat_axis=1, tiled=True)
    weights = first_block
    row_sums = contract_last(lax.all_gather(d_pre, "rep", axis=1, tiled=True), weights)
    d_rows = row_sums.astype(jnp.bfloat16)
    back_rows = relocate(d_rows.reshape(n_experts, capacity, feat_local)).reshape(
        rows_total, feat_local
    )
    row_grads = contract_first(placing, back_rows).reshape(tok_rows, top_k, feat_local)
    d_tokens = jnp.sum(row_grads, axis=1).astype(jnp.bfloat16)
    return (
        mixed,
        d_tokens,
        d_gates,
        grad_w_in[None],
        grad_bias_in[None],
        grad_w_out[None],
        grad_bias_out[None],
    )


def solution(mesh):
    return jax.shard_map(
        per_device,
        mesh=mesh,
        in_specs=(
            P(("node", "grp"), "rep"),
            P(("node", "grp"), None),
            P(("node", "grp"), None),
            P(("node", "grp"), None, "rep"),
            P(("node", "grp"), "rep"),
            P(("node", "grp"), "rep", None),
            P(("node", "grp"), "rep"),
            P(("node", "grp"), "rep"),
        ),
        out_specs=(
            P(("node", "grp"), "rep"),
            P(("node", "grp"), "rep"),
            P(("node", "grp"), None),
            P(("node", "grp"), None, "rep"),
            P(("node", "grp"), "rep"),
            P(("node", "grp"), "rep", None),
            P(("node", "grp"), "rep"),
        ),
        check_vma=False,
    )
```

profile of v0, /device:TPU:0, one launch (start us, length us, event | category | flops | bytes accessed | tf_op | source)
XLA Modules:
  0.0 130.0 jit_solution(18391526775065766837)
XLA Ops:
  7.2 0.9 copy.49
  8.3 0.8 copy.48
  9.5 0.3 convolution_convert_fusion.2
  9.8 0.8 copy.50
  10.6 7.3 %all-to-all-start = ((bf16[8,64,192]{2,1,0:T(8,128)(2,1)}), bf16[8,64,192]{2,1,0:T(8,128)(2,1)S(1)}, u32[]{:S(2)}, u32[]{:S(2)}) async-start(bf16[8,64,192]{2,1,0:T(8,128)(2,1)} %bitcast), calls=%async_computation | async-start | bytes 524288 | tf_op jit(solution)/shard_map/all_to_all | solution.py:20
  18.0 8.8 %all-to-all-done = bf16[8,64,192]{2,1,0:T(8,128)(2,1)S(1)} async-done(((bf16[8,64,192]{2,1,0:T(8,128)(2,1)}), bf16[8,64,192]{2,1,0:T(8,128)(2,1)S(1)}, u32[]{:S(2)}, u32[]{:S(2)}) %all-to-all-start) | async-done | bytes 196640 | tf_op jit(solution)/shard_map/all_to_all | solution.py:20
  27.0 8.6 %all_gather.12 = bf16[512,768]{0,1:T(8,128)(2,1)S(1)} all-gather(bf16[512,192]{0,1:T(8,128)(2,1)S(1)} %copy.51), channel_id=1, replica_groups=mesh['node'=4,'grp'=2,'rep'=4] {'rep'}, dimensions={1}, use_global_device_ids=true | all-gather | bytes 983040 | tf_op jit(solution)/shard_map/all_gather | solution.py:49
  35.6 1.8 %multiply_convert_fusion = (bf16[512,384]{1,0:T(8,128)(2,1)}, f32[512,384]{1,0:T(8,128)}) fusion(f32[384]{0:T(512)S(1)} %reduce.1, bf16[512,768]{0,1:T(8,128)(2,1)S(1)} %all_gather.12, bf16[1,768,384]{2,1,0:T(8,128)(2,1)S(1)} %copy-done.3), kind=kOutput, calls=%fused_computation.19 | convolution fusion | flops 303955968 | bytes 2557440 | tf_op jit(solution)/shard_map/dot_general | solution.py:50
  38.1 0.3 convolution_convert_fusion.1
  38.5 12.8 %all_to_all.58 = bf16[8,64,192]{2,1,0:T(8,128)(2,1)S(1)} all-to-all(bf16[8,64,192]{2,1,0:T(8,128)(2,1)S(1)} %bitcast.55), channel_id=1, replica_groups=mesh['node'=4,'grp'=2,'rep'=4] {'node','grp'}, dimensions={0} | all-to-all | bytes 393216 | tf_op jit(solution)/shard_map/all_to_all | solution.py:20
  51.5 7.8 %all_gather.14 = bf16[512,768]{0,1:T(8,128)(2,1)S(1)} all-gather(bf16[512,192]{0,1:T(8,128)(2,1)S(1)} %copy.60), channel_id=1, replica_groups=mesh['node'=4,'grp'=2,'rep'=4] {'rep'}, dimensions={1}, use_global_device_ids=true | all-gather | bytes 983040 | tf_op jit(solution)/shard_map/all_gather | solution.py:79
  59.3 2.9 %convert_reduce_fusion = (f32[384]{0:T(512)S(1)}, bf16[512,384]{1,0:T(8,128)(2,1)}) fusion(f32[512,384]{1,0:T(8,128)} %get-tuple-element.10, bf16[512,768]{0,1:T(8,128)(2,1)S(1)} %all_gather.14, bf16[1,384,768]{2,1,0:T(8,128)(2,1)S(1)} %copy-done.2), kind=kOutput, calls=%fused_computation.18 | convolution fusion | flops 306314880 | bytes 2557440 | tf_op jit(solution)/shard_map/dot_general | solution.py:14
  62.2 1.1 copy.52
  63.3 3.5 %all-to-all-start.1 = ((bf16[384,4,192]{0,2,1:T(8,128)(2,1)}), bf16[384,4,192]{0,2,1:T(8,128)(2,1)S(1)}, u32[]{:S(2)}, u32[]{:S(2)}) async-start(bf16[384,4,192]{0,2,1:T(8,128)(2,1)} %bitcast.3), calls=%async_computation.1 | async-start | bytes 1179648 | tf_op jit(solution)/shard_map/all_to_all | solution.py:53
  66.8 14.5 %all-to-all-done.1 = bf16[384,4,192]{0,2,1:T(8,128)(2,1)S(1)} async-done(((bf16[384,4,192]{0,2,1:T(8,128)(2,1)}), bf16[384,4,192]{0,2,1:T(8,128)(2,1)S(1)}, u32[]{:S(2)}, u32[]{:S(2)}) %all-to-all-start.1) | async-done | bytes 589856 | tf_op jit(solution)/shard_map/all_to_all | solution.py:53
  81.3 3.5 %all-to-all-start.4 = ((bf16[4,192,384]{2,1,0:T(8,128)(2,1)}), bf16[4,192,384]{2,1,0:T(8,128)(2,1)S(1)}, u32[]{:S(2)}, u32[]{:S(2)}) async-start(bf16[4,192,384]{2,1,0:T(8,128)(2,1)} %bitcast.56), calls=%async_computation.4 | async-start | bytes 1179648 | tf_op jit(solution)/shard_map/all_to_all | solution.py:86
  85.1 0.9 copy.70
  86.0 2.2 %fusion = bf16[512,192]{0,1:T(8,128)(2,1)S(1)} fusion(bf16[512,1536]{1,0:T(8,128)(2,1)} %all-gather.3.cloned.1.call-done, bf16[1536,192]{0,1:T(8,128)(2,1)} %bitcast.58, f32[192]{0:T(256)S(1)} %bitcast.61), kind=kOutput, calls=%fused_computation.5 | convolution fusion | flops 302186496 | bytes 2360064 | tf_op jit(solution)/shard_map/dot_general | solution.py:55
  88.2 0.8 copy.54
  89.1 5.2 %all-to-all-done.4 = bf16[4,192,384]{2,1,0:T(8,128)(2,1)S(1)} async-done(((bf16[4,192,384]{2,1,0:T(8,128)(2,1)}), bf16[4,192,384]{2,1,0:T(8,128)(2,1)S(1)}, u32[]{:S(2)}, u32[]{:S(2)}) %all-to-all-start.4) | async-done | bytes 589856 | tf_op jit(solution)/shard_map/all_to_all | solution.py:86
  94.3 4.8 %all-to-all-start.2 = ((bf16[8,64,192]{2,1,0:T(8,128)(2,1)}), bf16[8,64,192]{2,1,0:T(8,128)(2,1)}, u32[]{:S(2)}, u32[]{:S(2)}) async-start(bf16[8,64,192]{2,1,0:T(8,128)(2,1)} %bitcast.6), calls=%async_computation.2 | async-start | bytes 524288 | tf_op jit(solution)/shard_map/all_to_all | solution.py:20
  99.1 1.6 %convolution_bitcast_fusion.1 = f32[1,768,384]{2,1,0:T(8,128)} fusion(bf16[512,768]{0,1:T(8,128)(2,1)S(1)} %all_gather.12, bf16[512,384]{1,0:T(8,128)(2,1)S(1)} %copy-done.1), kind=kOutput, calls=%fused_computation.1 | convolution fusion | flops 301989888 | bytes 2359296 | tf_op jit(solution)/shard_map/dot_general | solution.py:8
  100.7 2.1 %convolution_convert_fusion = bf16[512,192]{0,1:T(8,128)(2,1)S(1)} fusion(bf16[512,1536]{1,0:T(8,128)(2,1)} %all-gather.5.cloned.1.call-done, bf16[192,1536]{1,0:T(8,128)(2,1)S(1)} %bitcast.57), kind=kOutput, calls=%fused_computation.4 | convolution fusion | flops 302088192 | bytes 2359296 | tf_op jit(solution)/shard_map/dot_general | solution.py:14
  102.9 0.8 copy.62
  103.7 4.1 %all-to-all-done.2 = bf16[8,64,192]{2,1,0:T(8,128)(2,1)} async-done(((bf16[8,64,192]{2,1,0:T(8,128)(2,1)}), bf16[8,64,192]{2,1,0:T(8,128)(2,1)}, u32[]{:S(2)}, u32[]{:S(2)}) %all-to-all-start.2) | async-done | bytes 196640 | tf_op jit(solution)/shard_map/all_to_all | solution.py:20
  107.8 3.6 %all-to-all-start.5 = ((bf16[8,64,192]{2,1,0:T(8,128)(2,1)}), bf16[8,64,192]{2,1,0:T(8,128)(2,1)S(1)}, u32[]{:S(2)}, u32[]{:S(2)}) async-start(bf16[8,64,192]{2,1,0:T(8,128)(2,1)} %bitcast.14), calls=%async_computation.5 | async-start | bytes 524288 | tf_op jit(solution)/shard_map/all_to_all | solution.py:20
  111.4 0.7 convert_reduce_fusion.1
  112.0 0.6 broadcast_in_dim.12
  112.6 1.5 %convolution_bitcast_fusion = f32[1,384,768]{2,1,0:T(8,128)} fusion(bf16[512,384]{1,0:T(8,128)(2,1)S(1)} %copy-done, bf16[512,768]{0,1:T(8,128)(2,1)S(1)} %all_gather.14), kind=kOutput, calls=%fused_computation | convolution fusion | flops 301989888 | bytes 2359296 | tf_op jit(solution)/shard_map/dot_general | solution.py:8
  114.1 1.9 %multiply_reduce_fusion = (f32[128,2]{0,1:T(2,128)S(1)}, bf16[128,192]{0,1:T(8,128)(2,1)}) fusion(f32[128,192]{0,1:T(8,128)S(1)} %convert_element_type.47, f32[128,2]{0,1:T(2,128)S(1)} %copy-done.6, bf16[512,192,1]{1,0,2:T(8,128)(2,1)} %bitcast.8, pred[128,2,512]{2,1,0:T(4,128)(4,1)S(1)} %eq.50), kind=kOutput, calls=%fused_computation.32 | convolution fusion | flops 50503424 | bytes 477184 | tf_op jit(solution)/shard_map/dot_general | solution.py:8
  116.0 6.3 %psum.7 = f32[128,2]{0,1:T(2,128)} all-reduce(f32[128,2]{0,1:T(2,128)S(1)} %get-tuple-element.7), channel_id=1, replica_groups=mesh['node'=4,'grp'=2,'rep'=4] {'rep'}, use_global_device_ids=true, to_apply=%region_4.0 | all-reduce | flops 256 | bytes 2048 | tf_op jit(solution)/shard_map/psum | solution.py:68
  122.3 0.9 convolution_reduce_fusion
  (41 shorter events, 2.1 us)
Async XLA Ops:
  7.2 10.8 %copy-start.5 = (f32[1,384]{1,0:T(1,128)S(1)}, f32[1,384]{1,0:T(1,128)}, u32[]{:S(2)}) copy-start(f32[1,384]{1,0:T(1,128)} %param.12) | copy-start | bytes 4612
  8.2 27.4 %copy-start.3 = (bf16[1,768,384]{2,1,0:T(8,128)(2,1)S(1)}, bf16[1,768,384]{2,1,0:T(8,128)(2,1)}, u32[]{:S(2)}) copy-start(bf16[1,768,384]{2,1,0:T(8,128)(2,1)} %param.11) | copy-start | bytes 1769476
  10.6 16.2 %all-to-all-start = ((bf16[8,64,192]{2,1,0:T(8,128)(2,1)}), bf16[8,64,192]{2,1,0:T(8,128)(2,1)S(1)}, u32[]{:S(2)}, u32[]{:S(2)}) async-start(bf16[8,64,192]{2,1,0:T(8,128)(2,1)} %bitcast), calls=%async_computation | async-start | bytes 524288 | tf_op jit(solution)/shard_map/all_to_all | solution.py:20
  17.9 68.1 %all-gather.3.cloned.1.call-start = ((), (), s32[]{:S(2)}) async-start(), calls=%async_computation.6 | async-start | bytes 1966080 | tf_op jit(solution)/shard_map/all_gather | solution.py:56
  35.6 1.8 %copy-start.6 = (f32[128,2]{0,1:T(2,128)S(1)}, f32[128,2]{0,1:T(2,128)}, u32[]{:S(2)}) copy-start(f32[128,2]{0,1:T(2,128)} %param.9) | copy-start | bytes 3076
  35.6 2.1 %copy-start.4 = (bf16[128,192]{0,1:T(8,128)(2,1)S(1)}, bf16[128,192]{0,1:T(8,128)(2,1)}, u32[]{:S(2)}) copy-start(bf16[128,192]{0,1:T(8,128)(2,1)} %param.15) | copy-start | bytes 147460
  37.3 63.4 %all-gather.5.cloned.1.call-start = ((), (), s32[]{:S(2)}) async-start(), calls=%async_computation.7 | async-start | bytes 1966080 | tf_op jit(solution)/shard_map/all_gather | solution.py:88
  38.1 21.3 %copy-start.2 = (bf16[1,384,768]{2,1,0:T(8,128)(2,1)S(1)}, bf16[1,384,768]{2,1,0:T(8,128)(2,1)}, u32[]{:S(2)}) copy-start(bf16[1,384,768]{2,1,0:T(8,128)(2,1)} %param.13) | copy-start | bytes 1769476
  63.3 18.0 %all-to-all-start.1 = ((bf16[384,4,192]{0,2,1:T(8,128)(2,1)}), bf16[384,4,192]{0,2,1:T(8,128)(2,1)S(1)}, u32[]{:S(2)}, u32[]{:S(2)}) async-start(bf16[384,4,192]{0,2,1:T(8,128)(2,1)} %bitcast.3), calls=%async_computation.1 | async-start | bytes 1179648 | tf_op jit(solution)/shard_map/all_to_all | solution.py:53
  66.8 19.2 %copy-start.7 = (f32[1,192]{1,0:T(1,128)S(1)}, f32[1,192]{1,0:T(1,128)}, u32[]{:S(2)}) copy-start(f32[1,192]{1,0:T(1,128)} %param.14) | copy-start | bytes 2308
  81.3 13.0 %all-to-all-start.4 = ((bf16[4,192,384]{2,1,0:T(8,128)(2,1)}), bf16[4,192,384]{2,1,0:T(8,128)(2,1)S(1)}, u32[]{:S(2)}, u32[]{:S(2)}) async-start(bf16[4,192,384]{2,1,0:T(8,128)(2,1)} %bitcast.56), calls=%async_computation.4 | async-start | bytes 1179648 | tf_op jit(solution)/shard_map/all_to_all | solution.py:86
  86.0 13.1 %copy-start.1 = (bf16[512,384]{1,0:T(8,128)(2,1)S(1)}, bf16[512,384]{1,0:T(8,128)(2,1)}, u32[]{:S(2)}) copy-start(bf16[512,384]{1,0:T(8,128)(2,1)} %get-tuple-element.12) | copy-start | bytes 1179652
  94.3 13.5 %all-to-all-start.2 = ((bf16[8,64,192]{2,1,0:T(8,128)(2,1)}), bf16[8,64,192]{2,1,0:T(8,128)(2,1)}, u32[]{:S(2)}, u32[]{:S(2)}) async-start(bf16[8,64,192]{2,1,0:T(8,128)(2,1)} %bitcast.6), calls=%async_computation.2 | async-start | bytes 524288 | tf_op jit(solution)/shard_map/all_to_all | solution.py:20
  100.7 11.9 %copy-start = (bf16[512,384]{1,0:T(8,128)(2,1)S(1)}, bf16[512,384]{1,0:T(8,128)(2,1)}, u32[]{:S(2)}) copy-start(bf16[512,384]{1,0:T(8,128)(2,1)} %get-tuple-element.9) | copy-start | bytes 1179652
  107.8 14.5 %all-to-all-start.5 = ((bf16[8,64,192]{2,1,0:T(8,128)(2,1)}), bf16[8,64,192]{2,1,0:T(8,128)(2,1)S(1)}, u32[]{:S(2)}, u32[]{:S(2)}) async-start(bf16[8,64,192]{2,1,0:T(8,128)(2,1)} %bitcast.14), calls=%async_computation.5 | async-start | bytes 524288 | tf_op jit(solution)/shard_map/all_to_all | solution.py:20
Sparse Core Ops, SparseCore 0:
  37.5 17.8 all-gather.2
  62.3 23.7 all-gather.4
where the time goes:
time: 131 us; the launch traced here: 130 us
  blocking collectives  35.6 us (27%)
  waiting for transfers between devices  32.7 us (25%)
  starting transfers between devices  22.7 us (17%)
  matrix products  15.4 us (12%)
  between operations  14.3 us (11%)
  local copies, waits for them, and re-layouts  8.35 us (6%)
    all_to_all x3, starting transfers between devices, relocate(): lax.all_to_all(buffer, ('node', 'grp'), split_axis=0, concat_axis=0, tile...  15.7 us
    all_to_all x1, waiting for transfers between devices, per_device(): lax.all_to_all(w_second, 'rep', split_axis=1, concat_axis=0, tiled=True)  14.5 us
    all_to_all x3, waiting for transfers between devices, relocate(): lax.all_to_all(buffer, ('node', 'grp'), split_axis=0, concat_axis=0, tile...  12.9 us
    all_to_all x1, blocking collectives, relocate(): lax.all_to_all(buffer, ('node', 'grp'), split_axis=0, concat_axis=0, tile...  12.8 us
    all_gather x1, blocking collectives, per_device(): full_x = lax.all_gather(expert_x, 'rep', axis=1, tiled=True)  8.6 us
    all_gather x1, blocking collectives, per_device(): full_grad = lax.all_gather(expert_grad, 'rep', axis=1, tiled=True)  7.84 us
    psum x1, blocking collectives, per_device(): d_gates = lax.psum(gate_terms, 'rep')  6.32 us
    dot_general x4, matrix products, contract_first(): lax.dot_general(left, right, (((0,), (0,)), ((), ())), preferred_element_...  5.86 us
  transfers between devices with their start and end apart: 7, of which 4 were waited for; matrix products, arithmetic and copies ran while one was open for 14% of the time, Pallas kernels for 0%

commit v1 on v0

--- a/solution.py
+++ b/solution.py
@@ -50,7 +50,10 @@
     pre_act = jnp.dot(full_x, w_first, preferred_element_type=jnp.float32)
     pre_act = pre_act + bias_first
     hidden = jax.nn.gelu(pre_act).astype(jnp.bfloat16)
-    second_block = lax.all_to_all(w_second, "rep", split_axis=1, concat_axis=0, tiled=True)
+    second_block = jnp.concatenate(
+        lax.all_to_all(jnp.stack(jnp.split(w_second, lax.axis_size("rep"), axis=1)), "rep", 0, 0),
+        axis=0,
+    )
     weights = second_block
     summed = jnp.dot(
         lax.all_gather(hidden, "rep", axis=1, tiled=True),

time: 131 us -> 131 us (level)
  no operation moved by 1% of the time
where the time goes in v1:
time: 131 us; the launch traced here: 130 us
  blocking collectives  35.6 us (27%)
  waiting for transfers between devices  32.9 us (25%)
  starting transfers between devices  22.7 us (17%)
  matrix products  15.4 us (12%)
  between operations  14.3 us (11%)
  local copies, waits for them, and re-layouts  7.66 us (6%)
  other arithmetic  1.93 us (1%)
    all_to_all x3, starting transfers between devices, relocate(): lax.all_to_all(buffer, ('node', 'grp'), split_axis=0, concat_axis=0, tile...  15.7 us
    all_to_all x1, waiting for transfers between devices, per_device(): lax.all_to_all(jnp.stack(jnp.split(w_second, lax.axis_size('rep'), axis=1...  14.7 us
    all_to_all x3, waiting for transfers between devices, relocate(): lax.all_to_all(buffer, ('node', 'grp'), split_axis=0, concat_axis=0, tile...  12.9 us
    all_to_all x1, blocking collectives, relocate(): lax.all_to_all(buffer, ('node', 'grp'), split_axis=0, concat_axis=0, tile...  12.8 us
    all_gather x1, blocking collectives, per_device(): full_x = lax.all_gather(expert_x, 'rep', axis=1, tiled=True)  8.6 us
    all_gather x1, blocking collectives, per_device(): full_grad = lax.all_gather(expert_grad, 'rep', axis=1, tiled=True)  7.84 us
    psum x1, blocking collectives, per_device(): d_gates = lax.psum(gate_terms, 'rep')  6.32 us
    dot_general x4, matrix products, contract_first(): lax.dot_general(left, right, (((0,), (0,)), ((), ())), preferred_element_...  5.86 us
  transfers between devices with their start and end apart: 7, of which 4 were waited for; matrix products, arithmetic and copies ran while one was open for 14% of the time, Pallas kernels for 0%

profile of v1, /device:TPU:0, one launch (start us, length us, event | category | flops | bytes accessed | tf_op | source)
XLA Modules:
  0.0 130.5 jit_solution(5463202274089670900)
XLA Ops:
  7.2 0.9 copy.63
  8.3 0.8 copy.62
  9.8 0.8 copy.64
  10.6 7.3 %all-to-all-start = ((bf16[8,64,192]{2,1,0:T(8,128)(2,1)}), bf16[8,64,192]{2,1,0:T(8,128)(2,1)S(1)}, u32[]{:S(2)}, u32[]{:S(2)}) async-start(bf16[8,64,192]{2,1,0:T(8,128)(2,1)} %bitcast), calls=%async_computation | async-start | bytes 524288 | tf_op jit(solution)/shard_map/all_to_all | solution.py:20
  18.0 8.8 %all-to-all-done = bf16[8,64,192]{2,1,0:T(8,128)(2,1)S(1)} async-done(((bf16[8,64,192]{2,1,0:T(8,128)(2,1)}), bf16[8,64,192]{2,1,0:T(8,128)(2,1)S(1)}, u32[]{:S(2)}, u32[]{:S(2)}) %all-to-all-start) | async-done | bytes 196640 | tf_op jit(solution)/shard_map/all_to_all | solution.py:20
  27.0 8.6 %all_gather.12 = bf16[512,768]{0,1:T(8,128)(2,1)S(1)} all-gather(bf16[512,192]{0,1:T(8,128)(2,1)S(1)} %copy.65), channel_id=1, replica_groups=mesh['node'=4,'grp'=2,'rep'=4] {'rep'}, dimensions={1}, use_global_device_ids=true | all-gather | bytes 983040 | tf_op jit(solution)/shard_map/all_gather | solution.py:49
  35.6 1.8 %multiply_convert_fusion = (bf16[512,384]{1,0:T(8,128)(2,1)}, f32[512,384]{1,0:T(8,128)}) fusion(f32[384]{0:T(512)S(1)} %reduce.1, bf16[512,768]{0,1:T(8,128)(2,1)S(1)} %all_gather.12, bf16[1,768,384]{2,1,0:T(8,128)(2,1)S(1)} %copy-done.3), kind=kOutput, calls=%fused_computation.19 | convolution fusion | flops 303955968 | bytes 2557440 | tf_op jit(solution)/shard_map/dot_general | solution.py:50
  38.1 0.3 convolution_convert_fusion.1
  38.5 12.8 %all_to_all.44 = bf16[8,64,192]{2,1,0:T(8,128)(2,1)S(1)} all-to-all(bf16[8,64,192]{2,1,0:T(8,128)(2,1)S(1)} %bitcast.63), channel_id=1, replica_groups=mesh['node'=4,'grp'=2,'rep'=4] {'node','grp'}, dimensions={0} | all-to-all | bytes 393216 | tf_op jit(solution)/shard_map/all_to_all | solution.py:20
  51.5 7.8 %all_gather.14 = bf16[512,768]{0,1:T(8,128)(2,1)S(1)} all-gather(bf16[512,192]{0,1:T(8,128)(2,1)S(1)} %copy.74), channel_id=1, replica_groups=mesh['node'=4,'grp'=2,'rep'=4] {'rep'}, dimensions={1}, use_global_device_ids=true | all-gather | bytes 983040 | tf_op jit(solution)/shard_map/all_gather | solution.py:82
  59.3 2.9 %convert_reduce_fusion = (f32[384]{0:T(512)S(1)}, bf16[512,384]{1,0:T(8,128)(2,1)}) fusion(f32[512,384]{1,0:T(8,128)} %get-tuple-element.14, bf16[512,768]{0,1:T(8,128)(2,1)S(1)} %all_gather.14, bf16[1,384,768]{2,1,0:T(8,128)(2,1)S(1)} %copy-done.2), kind=kOutput, calls=%fused_computation.18 | convolution fusion | flops 306314880 | bytes 2557440 | tf_op jit(solution)/shard_map/dot_general | solution.py:14
  62.2 0.3 copy.66
  62.6 0.9 pad_maximum_fusion
  63.5 3.5 %all-to-all-start.1 = ((bf16[4,384,192]{1,2,0:T(8,128)(2,1)}), bf16[4,384,192]{1,2,0:T(8,128)(2,1)S(1)}, u32[]{:S(2)}, u32[]{:S(2)}) async-start(bf16[4,384,192]{1,2,0:T(8,128)(2,1)} %pad_maximum_fusion), calls=%async_computation.1 | async-start | bytes 1179648 | tf_op jit(solution)/shard_map/all_to_all | solution.py:54
  67.0 14.7 %all-to-all-done.1 = bf16[4,384,192]{1,2,0:T(8,128)(2,1)S(1)} async-done(((bf16[4,384,192]{1,2,0:T(8,128)(2,1)}), bf16[4,384,192]{1,2,0:T(8,128)(2,1)S(1)}, u32[]{:S(2)}, u32[]{:S(2)}) %all-to-all-start.1) | async-done | bytes 589856 | tf_op jit(solution)/shard_map/all_to_all | solution.py:54
  81.8 3.5 %all-to-all-start.4 = ((bf16[4,192,384]{2,1,0:T(8,128)(2,1)}), bf16[4,192,384]{2,1,0:T(8,128)(2,1)S(1)}, u32[]{:S(2)}, u32[]{:S(2)}) async-start(bf16[4,192,384]{2,1,0:T(8,128)(2,1)} %bitcast.64), calls=%async_computation.4 | async-start | bytes 1179648 | tf_op jit(solution)/shard_map/all_to_all | solution.py:89
  85.6 0.9 copy.84
  86.4 2.2 %fusion = bf16[512,192]{0,1:T(8,128)(2,1)S(1)} fusion(bf16[512,1536]{1,0:T(8,128)(2,1)} %all-gather.3.cloned.1.call-done, bf16[1536,192]{0,1:T(8,128)(2,1)} %bitcast.66, f32[192]{0:T(256)S(1)} %bitcast.69), kind=kOutput, calls=%fused_computation.5 | convolution fusion | flops 302186496 | bytes 2360064 | tf_op jit(solution)/shard_map/dot_general | solution.py:58
  88.7 0.8 copy.68
  89.5 5.2 %all-to-all-done.4 = bf16[4,192,384]{2,1,0:T(8,128)(2,1)S(1)} async-done(((bf16[4,192,384]{2,1,0:T(8,128)(2,1)}), bf16[4,192,384]{2,1,0:T(8,128)(2,1)S(1)}, u32[]{:S(2)}, u32[]{:S(2)}) %all-to-all-start.4) | async-done | bytes 589856 | tf_op jit(solution)/shard_map/all_to_all | solution.py:89
  94.7 4.8 %all-to-all-start.2 = ((bf16[8,64,192]{2,1,0:T(8,128)(2,1)}), bf16[8,64,192]{2,1,0:T(8,128)(2,1)}, u32[]{:S(2)}, u32[]{:S(2)}) async-start(bf16[8,64,192]{2,1,0:T(8,128)(2,1)} %bitcast.9), calls=%async_computation.2 | async-start | bytes 524288 | tf_op jit(solution)/shard_map/all_to_all | solution.py:20
  99.5 1.6 %convolution_bitcast_fusion.1 = f32[1,768,384]{2,1,0:T(8,128)} fusion(bf16[512,768]{0,1:T(8,128)(2,1)S(1)} %all_gather.12, bf16[512,384]{1,0:T(8,128)(2,1)S(1)} %copy-done.1), kind=kOutput, calls=%fused_computation.1 | convolution fusion | flops 301989888 | bytes 2359296 | tf_op jit(solution)/shard_map/dot_general | solution.py:8
  101.2 2.1 %convolution_convert_fusion = bf16[512,192]{0,1:T(8,128)(2,1)S(1)} fusion(bf16[512,1536]{1,0:T(8,128)(2,1)} %all-gather.5.cloned.1.call-done, bf16[192,1536]{1,0:T(8,128)(2,1)S(1)} %bitcast.65), kind=kOutput, calls=%fused_computation.4 | convolution fusion | flops 302088192 | bytes 2359296 | tf_op jit(solution)/shard_map/dot_general | solution.py:14
  103.3 0.8 copy.76
  104.2 4.1 %all-to-all-done.2 = bf16[8,64,192]{2,1,0:T(8,128)(2,1)} async-done(((bf16[8,64,192]{2,1,0:T(8,128)(2,1)}), bf16[8,64,192]{2,1,0:T(8,128)(2,1)}, u32[]{:S(2)}, u32[]{:S(2)}) %all-to-all-start.2) | async-done | bytes 196640 | tf_op jit(solution)/shard_map/all_to_all | solution.py:20
  108.2 3.6 %all-to-all-start.5 = ((bf16[8,64,192]{2,1,0:T(8,128)(2,1)}), bf16[8,64,192]{2,1,0:T(8,128)(2,1)S(1)}, u32[]{:S(2)}, u32[]{:S(2)}) async-start(bf16[8,64,192]{2,1,0:T(8,128)(2,1)} %bitcast.16), calls=%async_computation.5 | async-start | bytes 524288 | tf_op jit(solution)/shard_map/all_to_all | solution.py:20
  111.8 0.7 convert_reduce_fusion.1
  112.5 0.6 broadcast_in_dim.12
  113.0 1.5 %convolution_bitcast_fusion = f32[1,384,768]{2,1,0:T(8,128)} fusion(bf16[512,384]{1,0:T(8,128)(2,1)S(1)} %copy-done, bf16[512,768]{0,1:T(8,128)(2,1)S(1)} %all_gather.14), kind=kOutput, calls=%fused_computation | convolution fusion | flops 301989888 | bytes 2359296 | tf_op jit(solution)/shard_map/dot_general | solution.py:8
  114.6 1.9 %multiply_reduce_fusion = (f32[128,2]{0,1:T(2,128)S(1)}, bf16[128,192]{0,1:T(8,128)(2,1)}) fusion(f32[128,192]{0,1:T(8,128)S(1)} %convert_element_type.47, f32[128,2]{0,1:T(2,128)S(1)} %copy-done.6, bf16[512,192,1]{1,0,2:T(8,128)(2,1)} %bitcast.11, pred[128,2,512]{2,1,0:T(4,128)(4,1)S(1)} %eq.50), kind=kOutput, calls=%fused_computation.33 | convolution fusion | flops 50503424 | bytes 477184 | tf_op jit(solution)/shard_map/dot_general | solution.py:8
  116.4 6.3 %psum.7 = f32[128,2]{0,1:T(2,128)} all-reduce(f32[128,2]{0,1:T(2,128)S(1)} %get-tuple-element.7), channel_id=1, replica_groups=mesh['node'=4,'grp'=2,'rep'=4] {'rep'}, use_global_device_ids=true, to_apply=%region_4.0 | all-reduce | flops 256 | bytes 2048 | tf_op jit(solution)/shard_map/psum | solution.py:71
  122.7 0.9 convolution_reduce_fusion
  (43 shorter events, 2.5 us)
Async XLA Ops:
  7.2 10.8 %copy-start.5 = (f32[1,384]{1,0:T(1,128)S(1)}, f32[1,384]{1,0:T(1,128)}, u32[]{:S(2)}) copy-start(f32[1,384]{1,0:T(1,128)} %param.12) | copy-start | bytes 4612
  8.2 27.4 %copy-start.3 = (bf16[1,768,384]{2,1,0:T(8,128)(2,1)S(1)}, bf16[1,768,384]{2,1,0:T(8,128)(2,1)}, u32[]{:S(2)}) copy-start(bf16[1,768,384]{2,1,0:T(8,128)(2,1)} %param.11) | copy-start | bytes 1769476
  10.6 16.2 %all-to-all-start = ((bf16[8,64,192]{2,1,0:T(8,128)(2,1)}), bf16[8,64,192]{2,1,0:T(8,128)(2,1)S(1)}, u32[]{:S(2)}, u32[]{:S(2)}) async-start(bf16[8,64,192]{2,1,0:T(8,128)(2,1)} %bitcast), calls=%async_computation | async-start | bytes 524288 | tf_op jit(solution)/shard_map/all_to_all | solution.py:20
  17.9 68.5 %all-gather.3.cloned.1.call-start = ((), (), s32[]{:S(2)}) async-start(), calls=%async_computation.6 | async-start | bytes 1966080 | tf_op jit(solution)/shard_map/all_gather | solution.py:59
  35.6 1.8 %copy-start.6 = (f32[128,2]{0,1:T(2,128)S(1)}, f32[128,2]{0,1:T(2,128)}, u32[]{:S(2)}) copy-start(f32[128,2]{0,1:T(2,128)} %param.9) | copy-start | bytes 3076
  35.6 2.1 %copy-start.4 = (bf16[128,192]{0,1:T(8,128)(2,1)S(1)}, bf16[128,192]{0,1:T(8,128)(2,1)}, u32[]{:S(2)}) copy-start(bf16[128,192]{0,1:T(8,128)(2,1)} %param.15) | copy-start | bytes 147460
  37.3 63.8 %all-gather.5.cloned.1.call-start = ((), (), s32[]{:S(2)}) async-start(), calls=%async_computation.7 | async-start | bytes 1966080 | tf_op jit(solution)/shard_map/all_gather | solution.py:91
  38.1 21.3 %copy-start.2 = (bf16[1,384,768]{2,1,0:T(8,128)(2,1)S(1)}, bf16[1,384,768]{2,1,0:T(8,128)(2,1)}, u32[]{:S(2)}) copy-start(bf16[1,384,768]{2,1,0:T(8,128)(2,1)} %param.13) | copy-start | bytes 1769476
  63.5 18.3 %all-to-all-start.1 = ((bf16[4,384,192]{1,2,0:T(8,128)(2,1)}), bf16[4,384,192]{1,2,0:T(8,128)(2,1)S(1)}, u32[]{:S(2)}, u32[]{:S(2)}) async-start(bf16[4,384,192]{1,2,0:T(8,128)(2,1)} %pad_maximum_fusion), calls=%async_computation.1 | async-start | bytes 1179648 | tf_op jit(solution)/shard_map/all_to_all | solution.py:54
  67.0 19.5 %copy-start.7 = (f32[1,192]{1,0:T(1,128)S(1)}, f32[1,192]{1,0:T(1,128)}, u32[]{:S(2)}) copy-start(f32[1,192]{1,0:T(1,128)} %param.14) | copy-start | bytes 2308
  81.8 13.0 %all-to-all-start.4 = ((bf16[4,192,384]{2,1,0:T(8,128)(2,1)}), bf16[4,192,384]{2,1,0:T(8,128)(2,1)S(1)}, u32[]{:S(2)}, u32[]{:S(2)}) async-start(bf16[4,192,384]{2,1,0:T(8,128)(2,1)} %bitcast.64), calls=%async_computation.4 | async-start | bytes 1179648 | tf_op jit(solution)/shard_map/all_to_all | solution.py:89
  86.4 13.1 %copy-start.1 = (bf16[512,384]{1,0:T(8,128)(2,1)S(1)}, bf16[512,384]{1,0:T(8,128)(2,1)}, u32[]{:S(2)}) copy-start(bf16[512,384]{1,0:T(8,128)(2,1)} %get-tuple-element.16) | copy-start | bytes 1179652
  94.7 13.5 %all-to-all-start.2 = ((bf16[8,64,192]{2,1,0:T(8,128)(2,1)}), bf16[8,64,192]{2,1,0:T(8,128)(2,1)}, u32[]{:S(2)}, u32[]{:S(2)}) async-start(bf16[8,64,192]{2,1,0:T(8,128)(2,1)} %bitcast.9), calls=%async_computation.2 | async-start | bytes 524288 | tf_op jit(solution)/shard_map/all_to_all | solution.py:20
  101.2 11.9 %copy-start = (bf16[512,384]{1,0:T(8,128)(2,1)S(1)}, bf16[512,384]{1,0:T(8,128)(2,1)}, u32[]{:S(2)}) copy-start(bf16[512,384]{1,0:T(8,128)(2,1)} %get-tuple-element.13) | copy-start | bytes 1179652
  108.2 14.5 %all-to-all-start.5 = ((bf16[8,64,192]{2,1,0:T(8,128)(2,1)}), bf16[8,64,192]{2,1,0:T(8,128)(2,1)S(1)}, u32[]{:S(2)}, u32[]{:S(2)}) async-start(bf16[8,64,192]{2,1,0:T(8,128)(2,1)} %bitcast.16), calls=%async_computation.5 | async-start | bytes 524288 | tf_op jit(solution)/shard_map/all_to_all | solution.py:20
Sparse Core Ops, SparseCore 0:
  37.5 17.8 all-gather.2
  62.3 24.0 all-gather.4
